TPU v7x, 32 devices: a whole 2x2x4 slice. The times are simulated.
32 devices in a mesh: gx: 8 (over y, x, core), gy: 4 (over z).
Axes of the slice: x: 2, y: 2, z: 4, core: 2. Of those that a mesh axis runs over, the one named last changes fastest.
Arguments:
- rhs_conc: float32 [16, 64, 2048], P('gx', 'gy'), may hold values from -60 to 60
- rhs_pots: float32 [16, 64, 33], P('gx', 'gy'), may hold values from -60 to 60
- diffusion: float32 [16, 64, 32], P('gx', 'gy'), may hold values from 0.05 to 5
- exchange: float32 [16, 64, 32], P('gx', 'gy'), may hold values from 0.2 to 4
- slope: float32 [16, 64, 32], P('gx', 'gy'), may hold values from 0.1 to 1
Outputs:
- sol_conc: float32 [16, 64, 2048], P('gx', 'gy')
- sol_pots: float32 [16, 64, 33], P('gx', 'gy')
All inputs are finite; a program needn't handle non-finite values.
Results may differ from a plain program's by a relative error of at most 0.0003.
Values sent between devices are 32-bit elements; how exact they have to be, the bound alone decides.
No kernel may reach another device: no remote copies, remote signals or barrier semaphores. Data moves between devices by JAX's collectives and lax.ppermute only.
A program may use at most 64 MiB of HBM per device.

v0:
```python
import jax
import jax.numpy as jnp
from jax import lax
from jax.sharding import PartitionSpec as P

ITERS = 10
node_cond = 1.0
plane_cond = 0.5
collector_cond = 2.0
epsilon = 1e-06


def padded_2(cells, sides, width):
    for axis, dim in sides:
        count = lax.axis_size(axis)
        ends = count - 1
        head = lax.slice_in_dim(cells, 0, width, axis=dim)
        tail = lax.slice_in_dim(cells, cells.shape[dim] - width, cells.shape[dim], axis=dim)
        cells = jnp.concatenate(
            [
                lax.ppermute(tail, axis, [(i, (i + 1) % count) for i in range(ends)]),
                cells,
                lax.ppermute(head, axis, [((i + 1) % count, i) for i in range(ends)]),
            ],
            axis=dim,
        )
    return cells


def mirror_laplace(values):
    inner = jnp.concatenate([values[..., :1], values[..., :-1]], axis=-1)
    outer = jnp.concatenate([values[..., 1:], values[..., -1:]], axis=-1)
    return 2.0 * values - inner - outer


def local_operator(conc, padded, diffusion, exchange, slope):
    nodes = exchange.shape[2]
    shell_count = conc.shape[2] // nodes
    shells = conc.reshape(conc.shape[0], conc.shape[1], nodes, shell_count)
    center = padded[1:-1, 1:-1]
    lateral = (
        4.0 * center - padded[2:, 1:-1] - padded[:-2, 1:-1] - padded[1:-1, 2:] - padded[1:-1, :-2]
    )
    node_pot = center[..., :nodes]
    collector = center[..., nodes]
    current = exchange * (node_pot - collector[..., None])
    surface = shells[..., shell_count - 1]
    surface_flag = (lax.broadcasted_iota(jnp.int32, (shell_count,), 0) == shell_count - 1).astype(
        jnp.float32
    )
    new_shells = (
        shells + diffusion[..., None] * mirror_laplace(shells) + current[..., None] * surface_flag
    )
    new_nodes = (
        node_cond * mirror_laplace(node_pot)
        + current
        - slope * surface
        + plane_cond * lateral[..., :nodes]
    )
    new_collector = collector_cond * lateral[..., nodes] - jnp.mean(current, axis=-1)
    return (
        new_shells.reshape(conc.shape),
        jnp.concatenate([new_nodes, new_collector[..., None]], axis=-1),
    )


def least_squares(columns, start_norm):
    count = len(columns)
    target = [start_norm] + [jnp.zeros_like(start_norm) for step in range(count)]
    cosines = []
    sines = []
    upper_rows = []
    for step in range(count):
        entries = list(columns[step])
        for row in range(step):
            first = cosines[row] * entries[row] + sines[row] * entries[row + 1]
            second = cosines[row] * entries[row + 1] - sines[row] * entries[row]
            entries[row] = first
            entries[row + 1] = second
        radius = jnp.sqrt(entries[step] * entries[step] + entries[step + 1] * entries[step + 1])
        cosine = entries[step] / radius
        sine = entries[step + 1] / radius
        entries[step] = radius
        cosines.append(cosine)
        sines.append(sine)
        lead = target[step]
        target[step] = cosine * lead
        target[step + 1] = -sine * lead
        upper_rows.append(entries[: step + 1])
    weights = [None] * count
    for row in range(count - 1, -1, -1):
        total = target[row]
        for later in range(row + 1, count):
            total = total - upper_rows[later][row] * weights[later]
        weights[row] = total / upper_rows[row][row]
    return weights


def shards(rhs_conc, rhs_pots, diffusion, exchange, slope):
    local_square = jnp.sum(rhs_conc * rhs_conc) + jnp.sum(rhs_pots * rhs_pots)
    start_norm = jnp.sqrt(lax.psum(local_square, ("gx", "gy")) + epsilon)
    basis = [(rhs_conc / start_norm, rhs_pots / start_norm)]
    columns = []
    for step in range(ITERS):
        padded = padded_2(basis[step][1], (("gx", 0), ("gy", 1)), 1)
        image_conc, image_pots = local_operator(basis[step][0], padded, diffusion, exchange, slope)
        local_dots = jnp.stack(
            [jnp.sum(vector[0] * image_conc) + jnp.sum(vector[1] * image_pots) for vector in basis]
        )
        image_square = jnp.sum(image_conc * image_conc) + jnp.sum(image_pots * image_pots)
        coeffs, total_square = lax.psum((local_dots, image_square), ("gx", "gy"))
        rest_conc, rest_pots = (image_conc, image_pots)
        for row in range(step + 1):
            rest_conc = rest_conc - coeffs[row] * basis[row][0]
            rest_pots = rest_pots - coeffs[row] * basis[row][1]
        height = jnp.sqrt(total_square - jnp.sum(coeffs * coeffs) + epsilon)
        basis.append((rest_conc / height, rest_pots / height))
        columns.append([coeffs[row] for row in range(step + 1)] + [height])
    weights = least_squares(columns, start_norm)
    sol_conc = weights[0] * basis[0][0]
    sol_pots = weights[0] * basis[0][1]
    for step in range(1, ITERS):
        sol_conc = sol_conc + weights[step] * basis[step][0]
        sol_pots = sol_pots + weights[step] * basis[step][1]
    return (sol_conc, sol_pots)


def solution(mesh):
    return jax.shard_map(
        shards,
        mesh=mesh,
        in_specs=(
            P("gx", "gy", None),
            P("gx", "gy", None),
            P("gx", "gy", None),
            P("gx", "gy", None),
            P("gx", "gy", None),
        ),
        out_specs=(P("gx", "gy", None), P("gx", "gy", None)),
        check_vma=False,
    )
```

profile of v0, /device:TPU:0, one launch (start us, length us, event | category | flops | bytes accessed | tf_op | source)
XLA Modules:
  0.0 950.6 jit_solution(5201951569017878183)
XLA Ops:
  2.0 1.7 multiply_reduce_fusion.65
  5.1 42.0 %psum.147 = f32[]{:T(128)} all-reduce(f32[]{:T(128)S(6)} %add.632), channel_id=1, replica_groups=mesh['gx'=8,'gy'=4] {'gx','gy'}, use_global_device_ids=true, to_apply=%region_2.0 | all-reduce | flops 1 | bytes 8 | tf_op jit(solution)/shard_map/psum | solution.py:101
  49.2 3.0 collective-permute-start.1
  57.7 4.5 collective-permute-start.3
  62.7 1.5 collective-permute-done.3
  69.2 42.0 %all-reduce.9 = (f32[]{:T(128)}, f32[1]{0:T(128)}) all-reduce(f32[]{:T(128)S(6)} %add.639, f32[1]{0:T(128)} %bitcast.3), channel_id=1, replica_groups=mesh['gx'=8,'gy'=4] {'gx','gy'}, use_global_device_ids=true, to_apply=%region_9.0 | all-reduce | flops 2 | bytes 16 | tf_op jit(solution)/shard_map/psum | solution.py:111
  116.6 3.0 collective-permute-start.5
  124.6 4.5 collective-permute-start.7
  129.5 1.5 collective-permute-done.7
  137.5 42.3 %all-reduce.8 = (f32[]{:T(128)}, f32[2]{0:T(128)S(1)}) all-reduce(f32[]{:T(128)S(6)} %add.649, f32[2]{0:T(128)S(1)} %pad_maximum_fusion.120), channel_id=1, replica_groups=mesh['gx'=8,'gy'=4] {'gx','gy'}, use_global_device_ids=true, to_apply=%region_18.0 | all-reduce | flops 3 | bytes 24 | tf_op jit(solution)/shard_map/psum | solution.py:111
  187.5 3.0 collective-permute-start.9
  196.1 4.7 collective-permute-start.11
  210.8 41.6 %all-reduce.7 = (f32[]{:T(128)}, f32[3]{0:T(128)S(1)}) all-reduce(f32[]{:T(128)S(6)} %add.660, f32[3]{0:T(128)S(1)} %pad_maximum_fusion.121), channel_id=1, replica_groups=mesh['gx'=8,'gy'=4] {'gx','gy'}, use_global_device_ids=true, to_apply=%region_30.0 | all-reduce | flops 4 | bytes 32 | tf_op jit(solution)/shard_map/psum | solution.py:111
  255.0 1.9 subtract_divide_fusion.15
  258.1 1.9 subtract_divide_fusion.6
  262.0 3.0 collective-permute-start.13
  271.7 4.5 collective-permute-start.15
  287.7 41.9 %all-reduce.6 = (f32[]{:T(128)}, f32[4]{0:T(128)S(1)}) all-reduce(f32[]{:T(128)S(6)} %add.672, f32[4]{0:T(128)S(1)} %pad_maximum_fusion.122), channel_id=1, replica_groups=mesh['gx'=8,'gy'=4] {'gx','gy'}, use_global_device_ids=true, to_apply=%region_44.0 | all-reduce | flops 5 | bytes 40 | tf_op jit(solution)/shard_map/psum | solution.py:111
  332.2 2.6 subtract_divide_fusion.14
  336.7 2.7 subtract_divide_fusion.5
  341.3 3.0 collective-permute-start.17
  353.1 4.5 collective-permute-start.19
  358.1 1.5 collective-permute-done.19
  370.5 41.6 %all-reduce.5 = (f32[]{:T(128)}, f32[5]{0:T(128)S(1)}) all-reduce(f32[]{:T(128)S(6)} %add.685, f32[5]{0:T(128)S(1)} %stack.210), channel_id=1, replica_groups=mesh['gx'=8,'gy'=4] {'gx','gy'}, use_global_device_ids=true, to_apply=%region_60.0 | all-reduce | flops 6 | bytes 48 | tf_op jit(solution)/shard_map/psum | solution.py:111
  414.7 3.2 subtract_divide_fusion.13
  419.1 3.2 subtract_divide_fusion.4
  424.3 3.2 collective-permute-start.21
  438.2 4.5 collective-permute-start.23
  456.9 41.9 %all-reduce.4 = (f32[]{:T(128)}, f32[6]{0:T(128)S(1)}) all-reduce(f32[]{:T(128)S(6)} %add.699, f32[6]{0:T(128)S(1)} %stack.217), channel_id=1, replica_groups=mesh['gx'=8,'gy'=4] {'gx','gy'}, use_global_device_ids=true, to_apply=%region_78.0 | all-reduce | flops 7 | bytes 56 | tf_op jit(solution)/shard_map/psum | solution.py:111
  501.4 3.7 subtract_divide_fusion.12
  506.9 3.8 subtract_divide_fusion.3
  515.4 3.0 collective-permute-start.25
  530.8 4.5 collective-permute-start.27
  539.8 1.7 multiply_reduce_fusion.31
  551.5 41.6 %all-reduce.3 = (f32[]{:T(128)}, f32[7]{0:T(128)S(1)}) all-reduce(f32[]{:T(128)S(6)} %add.714, f32[7]{0:T(128)S(1)} %stack.225), channel_id=1, replica_groups=mesh['gx'=8,'gy'=4] {'gx','gy'}, use_global_device_ids=true, to_apply=%region_98.0 | all-reduce | flops 8 | bytes 64 | tf_op jit(solution)/shard_map/psum | solution.py:111
  595.8 4.4 subtract_divide_fusion.11
  602.2 4.5 subtract_divide_fusion.2
  611.8 2.1 copy.529
  615.2 3.6 collective-permute-start.29
  618.8 2.1 pad_maximum_fusion.15
  632.6 4.8 collective-permute-start.31
  645.6 2.6 multiply_reduce_fusion.22
  659.6 40.8 %all-reduce.2 = (f32[]{:T(128)}, f32[8]{0:T(128)S(1)}) all-reduce(f32[]{:T(128)S(6)} %add.730, f32[8]{0:T(128)S(1)} %stack.234), channel_id=1, replica_groups=mesh['gx'=8,'gy'=4] {'gx','gy'}, use_global_device_ids=true, to_apply=%region_120.0 | all-reduce | flops 9 | bytes 72 | tf_op jit(solution)/shard_map/psum | solution.py:111
  703.1 5.0 subtract_divide_fusion.10
  710.7 5.1 subtract_divide_fusion.1
  723.4 2.1 copy.530
  726.8 3.6 collective-permute-start.33
  730.4 2.1 pad_maximum_fusion.17
  738.6 1.9 concatenate.447
  743.7 4.5 collective-permute-start.35
  755.7 1.7 multiply_reduce_fusion.78
  757.3 2.1 multiply_reduce_fusion.12
  772.0 41.0 %all-reduce.1 = (f32[]{:T(128)}, f32[9]{0:T(128)S(1)}) all-reduce(f32[]{:T(128)S(6)} %add.747, f32[9]{0:T(128)S(1)} %stack.244), channel_id=1, replica_groups=mesh['gx'=8,'gy'=4] {'gx','gy'}, use_global_device_ids=true, to_apply=%region_144.0 | all-reduce | flops 10 | bytes 80 | tf_op jit(solution)/shard_map/psum | solution.py:111
  815.7 5.7 subtract_divide_fusion.9
  824.0 6.6 subtract_divide_fusion
  839.7 2.1 copy.531
  843.1 3.6 collective-permute-start.37
  846.8 2.0 pad_maximum_fusion.19
  856.9 1.9 concatenate.461
  861.6 4.5 collective-permute-start.39
  872.2 2.0 mul.2912
  874.2 1.7 multiply_reduce_fusion.66
  875.9 2.1 multiply_reduce_fusion
  891.7 40.8 %all-reduce = (f32[10]{0:T(128)S(1)}, f32[]{:T(128)}) all-reduce(f32[10]{0:T(128)S(1)} %stack.255, f32[]{:T(128)S(6)} %add.765), channel_id=1, replica_groups=mesh['gx'=8,'gy'=4] {'gx','gy'}, use_global_device_ids=true, to_apply=%region_167.0 | all-reduce | flops 11 | bytes 88 | tf_op jit(solution)/shard_map/psum | solution.py:111
  (492 shorter events, 152.6 us)
Async XLA Ops:
  0.6 4.4 copy-start.43
  2.0 50.2 %copy-start = (f32[2,16,2048]{2,1,0:T(8,128)S(1)}, f32[2,16,2048]{2,1,0:T(8,128)}, u32[]{:S(2)}) copy-start(f32[2,16,2048]{2,1,0:T(8,128)} %param.5) | copy-start | bytes 786436
  47.9 8.4 collective-permute-start
  49.2 7.1 collective-permute-start.1
  56.4 6.2 collective-permute-start.2
  57.7 6.5 collective-permute-start.3
  115.3 7.8 collective-permute-start.4
  116.6 6.5 collective-permute-start.5
  123.3 6.2 collective-permute-start.6
  124.6 6.5 collective-permute-start.7
  186.2 8.4 collective-permute-start.8
  187.5 7.1 collective-permute-start.9
  194.8 6.4 collective-permute-start.10
  196.1 6.5 collective-permute-start.11
  260.7 9.5 collective-permute-start.12
  262.0 8.2 collective-permute-start.13
  270.4 6.2 collective-permute-start.14
  271.7 6.5 collective-permute-start.15
  340.0 11.7 %collective-permute-start.16 = (f32[1,16,33]{1,0,2:T(1,128)}, f32[1,16,33]{1,0,2:T(1,128)S(1)}, u32[]{:S(2)}, u32[]{:S(2)}) collective-permute-start(f32[1,16,33]{1,0,2:T(1,128)} %get-tuple-element.304), channel_id=1, source_target_pairs={{4,0},{8,4},{12,8},{16,12},{20,16},{24,20},{28,24},{5,1},{9,5},{13... | collective-permute-start | bytes 6344 | tf_op jit(solution)/shard_map/ppermute | solution.py:23
  341.3 10.4 %collective-permute-start.17 = (f32[1,16,33]{1,0,2:T(1,128)}, f32[1,16,33]{1,0,2:T(1,128)S(1)}, u32[]{:S(2)}, u32[]{:S(2)}) collective-permute-start(f32[1,16,33]{1,0,2:T(1,128)} %get-tuple-element.303), channel_id=1, source_target_pairs={{0,4},{4,8},{8,12},{12,16},{16,20},{20,24},{24,28},{1,5},{5,9},{9,... | collective-permute-start | bytes 6344 | tf_op jit(solution)/shard_map/ppermute | solution.py:21
  351.8 6.2 collective-permute-start.18
  353.1 6.5 collective-permute-start.19
  423.0 13.7 %collective-permute-start.20 = (f32[1,16,33]{1,0,2:T(1,128)S(1)}, f32[1,16,33]{1,0,2:T(1,128)S(1)}, u32[]{:S(2)}, u32[]{:S(2)}) collective-permute-start(f32[1,16,33]{1,0,2:T(1,128)S(1)} %get-tuple-element.297), channel_id=1, source_target_pairs={{4,0},{8,4},{12,8},{16,12},{20,16},{24,20},{28,24},{5,1},{9,5},{13... | collective-permute-start | bytes 6344 | tf_op jit(solution)/shard_map/ppermute | solution.py:23
  424.3 12.4 %collective-permute-start.21 = (f32[1,16,33]{1,0,2:T(1,128)S(1)}, f32[1,16,33]{1,0,2:T(1,128)S(1)}, u32[]{:S(2)}, u32[]{:S(2)}) collective-permute-start(f32[1,16,33]{1,0,2:T(1,128)S(1)} %get-tuple-element.296), channel_id=1, source_target_pairs={{0,4},{4,8},{8,12},{12,16},{16,20},{20,24},{24,28},{1,5},{5,9},{9,... | collective-permute-start | bytes 6344 | tf_op jit(solution)/shard_map/ppermute | solution.py:21
  429.8 6.7 copy-start.9
  436.9 6.2 collective-permute-start.22
  438.2 6.5 collective-permute-start.23
  443.1 1.9 copy-start.40
  514.1 15.2 %collective-permute-start.24 = (f32[1,16,33]{1,0,2:T(1,128)}, f32[1,16,33]{1,0,2:T(1,128)S(1)}, u32[]{:S(2)}, u32[]{:S(2)}) collective-permute-start(f32[1,16,33]{1,0,2:T(1,128)} %get-tuple-element.289), channel_id=1, source_target_pairs={{4,0},{8,4},{12,8},{16,12},{20,16},{24,20},{28,24},{5,1},{9,5},{13... | collective-permute-start | bytes 6344 | tf_op jit(solution)/shard_map/ppermute | solution.py:23
  515.4 13.9 %collective-permute-start.25 = (f32[1,16,33]{1,0,2:T(1,128)}, f32[1,16,33]{1,0,2:T(1,128)S(1)}, u32[]{:S(2)}, u32[]{:S(2)}) collective-permute-start(f32[1,16,33]{1,0,2:T(1,128)} %get-tuple-element.288), channel_id=1, source_target_pairs={{0,4},{4,8},{8,12},{12,16},{16,20},{20,24},{24,28},{1,5},{5,9},{9,... | collective-permute-start | bytes 6344 | tf_op jit(solution)/shard_map/ppermute | solution.py:21
  529.5 6.2 collective-permute-start.26
  530.8 6.5 collective-permute-start.27
  535.7 1.9 copy-start.37
  535.7 1.9 copy-start.38
  595.8 6.4 copy-start.23
  609.2 9.5 %copy-start.3 = (f32[2,16,32,1]{3,2,1,0:T(8,128)S(1)}, f32[2,16,32,1]{3,2,1,0:T(8,128)}, u32[]{:S(2)}) copy-start(f32[2,16,32,1]{3,2,1,0:T(8,128)} %get-tuple-element.197) | copy-start | bytes 12292
  613.9 16.6 %collective-permute-start.28 = (f32[1,16,33]{1,0,2:T(1,128)}, f32[1,16,33]{1,0,2:T(1,128)S(1)}, u32[]{:S(2)}, u32[]{:S(2)}) collective-permute-start(f32[1,16,33]{1,0,2:T(1,128)} %get-tuple-element.280), channel_id=1, source_target_pairs={{4,0},{8,4},{12,8},{16,12},{20,16},{24,20},{28,24},{5,1},{9,5},{13... | collective-permute-start | bytes 6344 | tf_op jit(solution)/shard_map/ppermute | solution.py:23
  615.2 15.3 %collective-permute-start.29 = (f32[1,16,33]{1,0,2:T(1,128)}, f32[1,16,33]{1,0,2:T(1,128)}, u32[]{:S(2)}, u32[]{:S(2)}) collective-permute-start(f32[1,16,33]{1,0,2:T(1,128)} %get-tuple-element.279), channel_id=1, source_target_pairs={{0,4},{4,8},{8,12},{12,16},{16,20},{20,24},{24,28},{1,5},{5,9},{9,... | collective-permute-start | bytes 6344 | tf_op jit(solution)/shard_map/ppermute | solution.py:21
  618.8 2.1 copy-start.12
  618.8 2.1 copy-start.13
  621.9 7.6 copy-start.8
  631.3 7.2 collective-permute-start.30
  632.6 7.0 collective-permute-start.31
  638.5 2.2 copy-start.28
  638.5 2.2 copy-start.35
  638.5 2.2 copy-start.36
  703.1 7.6 copy-start.19
  718.4 12.0 %copy-start.2 = (f32[2,16,32,1]{3,2,1,0:T(8,128)S(1)}, f32[2,16,32,1]{3,2,1,0:T(8,128)}, u32[]{:S(2)}) copy-start(f32[2,16,32,1]{3,2,1,0:T(8,128)} %get-tuple-element.193) | copy-start | bytes 12292
  725.5 16.0 %collective-permute-start.32 = (f32[1,16,33]{1,0,2:T(1,128)}, f32[1,16,33]{1,0,2:T(1,128)}, u32[]{:S(2)}, u32[]{:S(2)}) collective-permute-start(f32[1,16,33]{1,0,2:T(1,128)} %get-tuple-element.270), channel_id=1, source_target_pairs={{4,0},{8,4},{12,8},{16,12},{20,16},{24,20},{28,24},{5,1},{9,5},{13... | collective-permute-start | bytes 6344 | tf_op jit(solution)/shard_map/ppermute | solution.py:23
  726.8 14.7 %collective-permute-start.33 = (f32[1,16,33]{1,0,2:T(1,128)}, f32[1,16,33]{1,0,2:T(1,128)}, u32[]{:S(2)}, u32[]{:S(2)}) collective-permute-start(f32[1,16,33]{1,0,2:T(1,128)} %get-tuple-element.269), channel_id=1, source_target_pairs={{0,4},{4,8},{8,12},{12,16},{16,20},{20,24},{24,28},{1,5},{5,9},{9,... | collective-permute-start | bytes 6344 | tf_op jit(solution)/shard_map/ppermute | solution.py:21
  730.4 2.1 copy-start.10
  730.4 2.1 copy-start.11
  733.6 7.0 copy-start.7
  742.4 7.7 collective-permute-start.34
  743.7 7.0 collective-permute-start.35
  771.9 43.8 %copy-start.24 = (f32[2,16,32]{1,0,2:T(2,128)S(1)}, f32[2,16,32]{1,0,2:T(2,128)}, u32[]{:S(2)}) copy-start(f32[2,16,32]{1,0,2:T(2,128)} %get-tuple-element.161) | copy-start | bytes 12292
  821.4 2.0 copy-start.5
  834.1 12.7 %copy-start.1 = (f32[2,16,32,1]{3,2,1,0:T(8,128)S(1)}, f32[2,16,32,1]{3,2,1,0:T(8,128)}, u32[]{:S(2)}) copy-start(f32[2,16,32,1]{3,2,1,0:T(8,128)} %get-tuple-element.189) | copy-start | bytes 12292
  841.9 17.0 %collective-permute-start.36 = (f32[1,16,33]{1,0,2:T(1,128)}, f32[1,16,33]{1,0,2:T(1,128)}, u32[]{:S(2)}, u32[]{:S(2)}) collective-permute-start(f32[1,16,33]{1,0,2:T(1,128)} %get-tuple-element.259), channel_id=1, source_target_pairs={{4,0},{8,4},{12,8},{16,12},{20,16},{24,20},{28,24},{5,1},{9,5},{13... | collective-permute-start | bytes 6344 | tf_op jit(solution)/shard_map/ppermute | solution.py:23
  843.1 15.7 %collective-permute-start.37 = (f32[1,16,33]{1,0,2:T(1,128)}, f32[1,16,33]{1,0,2:T(1,128)}, u32[]{:S(2)}, u32[]{:S(2)}) collective-permute-start(f32[1,16,33]{1,0,2:T(1,128)} %get-tuple-element.258), channel_id=1, source_target_pairs={{0,4},{4,8},{8,12},{12,16},{16,20},{20,24},{24,28},{1,5},{5,9},{9,... | collective-permute-start | bytes 6344 | tf_op jit(solution)/shard_map/ppermute | solution.py:21
  856.9 1.9 copy-start.6
  860.3 7.7 collective-permute-start.38
  861.6 7.0 collective-permute-start.39
  872.2 3.7 copy-start.20
  (39 other events, 45.7 us)
where the time goes:
time: 965 us; the launch traced here: 951 us
  blocking collectives  457 us (47%)
  between operations  171 us (18%)
  other arithmetic  118 us (12%)
  starting transfers between devices  104 us (11%)
  local copies, waits for them, and re-layouts  87.2 us (9%)
  waiting for transfers between devices  12.9 us (1%)
    psum x10, blocking collectives, shards(): coeffs, total_square = lax.psum((local_dots, image_square), ('gx', 'gy'))  415 us
    ppermute x20, starting transfers between devices, padded_2(): lax.ppermute(tail, axis, [(i, (i + 1) % count) for i in range(ends)])  78.2 us
    div x18, other arithmetic, shards(): basis.append((rest_conc / height, rest_pots / height))  58.3 us
    psum x1, blocking collectives, shards(): start_norm = jnp.sqrt(lax.psum(local_square, ('gx', 'gy')) + epsilon)  42 us
    ppermute x20, starting transfers between devices, padded_2(): lax.ppermute(head, axis, [((i + 1) % count, i) for i in range(ends)])  25.8 us
  transfers between devices with their start and end apart: 40, of which 10 were waited for; matrix products, arithmetic and copies ran while one was open for 4% of the time, Pallas kernels for 0%

commit v1 on v0

--- a/solution.py
+++ b/solution.py
@@ -8,6 +8,14 @@
 plane_cond = 0.5
 collector_cond = 2.0
 epsilon = 1e-06
+
+
+def _place_strings(my_tile):
+    which_axis = "gy"
+    axis_tag = "gx"
+    for u in (which_axis, axis_tag):
+        my_tile = lax.psum(my_tile, u)
+    return my_tile
 
 
 def padded_2(cells, sides, width):
@@ -108,7 +116,7 @@
             [jnp.sum(vector[0] * image_conc) + jnp.sum(vector[1] * image_pots) for vector in basis]
         )
         image_square = jnp.sum(image_conc * image_conc) + jnp.sum(image_pots * image_pots)
-        coeffs, total_square = lax.psum((local_dots, image_square), ("gx", "gy"))
+        coeffs, total_square = _place_strings((local_dots, image_square))
         rest_conc, rest_pots = (image_conc, image_pots)
         for row in range(step + 1):
             rest_conc = rest_conc - coeffs[row] * basis[row][0]

time: 965 us -> 791 us (0.82)
  blocking collectives: 457 us -> 282 us
    psum x10 -> x20, blocking collectives: 415 us -> 240 us  [_place_strings(): my_tile = lax.psum(my_tile, u)]
  transfers between devices with their start and end apart: 40 -> 40, of which waited for: 10 -> 15; matrix products, arithmetic and copies ran while one was open for 4% -> 5% of each run, Pallas kernels for 0% -> 0%
where the time goes in v1:
time: 791 us; the launch traced here: 776 us
  blocking collectives  282 us (36%)
  between operations  171 us (22%)
  other arithmetic  118 us (15%)
  starting transfers between devices  104 us (13%)
  local copies, waits for them, and re-layouts  87.2 us (11%)
  waiting for transfers between devices  14.5 us (2%)
    psum x20, blocking collectives, _place_strings(): my_tile = lax.psum(my_tile, u)  240 us
    ppermute x20, starting transfers between devices, padded_2(): lax.ppermute(tail, axis, [(i, (i + 1) % count) for i in range(ends)])  77.8 us
    div x18, other arithmetic, shards(): basis.append((rest_conc / height, rest_pots / height))  58.3 us
    psum x1, blocking collectives, shards(): start_norm = jnp.sqrt(lax.psum(local_square, ('gx', 'gy')) + epsilon)  42 us
    ppermute x20, starting transfers between devices, padded_2(): lax.ppermute(head, axis, [((i + 1) % count, i) for i in range(ends)])  25.8 us
    unnamed x139, local copies, waits for them, and re-layouts  18.5 us
  transfers between devices with their start and end apart: 40, of which 15 were waited for; matrix products, arithmetic and copies ran while one was open for 5% of the time, Pallas kernels for 0%

profile of v1, /device:TPU:0, one launch (start us, length us, event | category | flops | bytes accessed | tf_op | source)
XLA Modules:
  0.0 776.1 jit_solution(11603291778760787407)
XLA Ops:
  5.1 42.0 %psum.287 = f32[]{:T(128)} all-reduce(f32[]{:T(128)S(6)} %add.672), channel_id=1, replica_groups=mesh['gx'=8,'gy'=4] {'gx','gy'}, use_global_device_ids=true, to_apply=%region_2.0 | all-reduce | flops 1 | bytes 8 | tf_op jit(solution)/shard_map/psum | solution.py:109
  49.2 3.0 collective-permute-start.1
  57.7 4.5 collective-permute-start.3
  69.2 13.7 %all-reduce.19 = (f32[]{:T(128)}, f32[1]{0:T(128)}) all-reduce(f32[]{:T(128)S(6)} %add.679, f32[1]{0:T(128)} %bitcast.3), channel_id=1, replica_groups=mesh['gx'=8,'gy'=4] {'gy'}, use_global_device_ids=true, to_apply=%region_10.0 | all-reduce | flops 2 | bytes 16 | tf_op jit(solution)/shard_map/psum | solution.py:17
  82.9 12.4 %all-reduce.9 = (f32[]{:T(128)}, f32[1]{0:T(128)}) all-reduce(f32[]{:T(128)} %get-tuple-element.177, f32[1]{0:T(128)} %get-tuple-element.178), channel_id=1, replica_groups=mesh['gx'=8,'gy'=4] {'gx'}, use_global_device_ids=true, to_apply=%region_11.0 | all-reduce | flops 2 | bytes 16 | tf_op jit(solution)/shard_map/psum | solution.py:17
  100.7 3.0 collective-permute-start.5
  108.6 4.5 collective-permute-start.7
  122.0 11.4 %all-reduce.18 = (f32[]{:T(128)}, f32[2]{0:T(128)S(1)}) all-reduce(f32[]{:T(128)S(6)} %add.689, f32[2]{0:T(128)S(1)} %pad_maximum_fusion.120), channel_id=1, replica_groups=mesh['gx'=8,'gy'=4] {'gy'}, use_global_device_ids=true, to_apply=%region_21.0 | all-reduce | flops 3 | bytes 24 | tf_op jit(solution)/shard_map/psum | solution.py:17
  133.4 12.4 %all-reduce.8 = (f32[]{:T(128)}, f32[2]{0:T(128)S(1)}) all-reduce(f32[]{:T(128)} %get-tuple-element.175, f32[2]{0:T(128)S(1)} %get-tuple-element.176), channel_id=1, replica_groups=mesh['gx'=8,'gy'=4] {'gx'}, use_global_device_ids=true, to_apply=%region_22.0 | all-reduce | flops 3 | bytes 24 | tf_op jit(solution)/shard_map/psum | solution.py:17
  153.5 3.0 collective-permute-start.9
  162.0 4.5 collective-permute-start.11
  177.2 11.3 %all-reduce.17 = (f32[]{:T(128)}, f32[3]{0:T(128)S(1)}) all-reduce(f32[]{:T(128)S(6)} %add.700, f32[3]{0:T(128)S(1)} %pad_maximum_fusion.121), channel_id=1, replica_groups=mesh['gx'=8,'gy'=4] {'gy'}, use_global_device_ids=true, to_apply=%region_35.0 | all-reduce | flops 4 | bytes 32 | tf_op jit(solution)/shard_map/psum | solution.py:17
  188.6 12.9 %all-reduce.7 = (f32[]{:T(128)}, f32[3]{0:T(128)S(1)}) all-reduce(f32[]{:T(128)} %get-tuple-element.173, f32[3]{0:T(128)S(1)} %get-tuple-element.174), channel_id=1, replica_groups=mesh['gx'=8,'gy'=4] {'gx'}, use_global_device_ids=true, to_apply=%region_36.0 | all-reduce | flops 4 | bytes 32 | tf_op jit(solution)/shard_map/psum | solution.py:17
  211.0 3.0 collective-permute-start.13
  220.7 4.5 collective-permute-start.15
  237.2 11.3 %all-reduce.16 = (f32[]{:T(128)}, f32[4]{0:T(128)S(1)}) all-reduce(f32[]{:T(128)S(6)} %add.712, f32[4]{0:T(128)S(1)} %pad_maximum_fusion.122), channel_id=1, replica_groups=mesh['gx'=8,'gy'=4] {'gy'}, use_global_device_ids=true, to_apply=%region_51.0 | all-reduce | flops 5 | bytes 40 | tf_op jit(solution)/shard_map/psum | solution.py:17
  248.5 12.4 %all-reduce.6 = (f32[]{:T(128)}, f32[4]{0:T(128)S(1)}) all-reduce(f32[]{:T(128)} %get-tuple-element.171, f32[4]{0:T(128)S(1)} %get-tuple-element.172), channel_id=1, replica_groups=mesh['gx'=8,'gy'=4] {'gx'}, use_global_device_ids=true, to_apply=%region_52.0 | all-reduce | flops 5 | bytes 40 | tf_op jit(solution)/shard_map/psum | solution.py:17
  263.6 2.6 subtract_divide_fusion.14
  268.0 2.7 subtract_divide_fusion.5
  272.6 3.0 collective-permute-start.17
  284.5 4.5 collective-permute-start.19
  302.4 11.3 %all-reduce.15 = (f32[]{:T(128)}, f32[5]{0:T(128)S(1)}) all-reduce(f32[]{:T(128)S(6)} %add.725, f32[5]{0:T(128)S(1)} %stack.210), channel_id=1, replica_groups=mesh['gx'=8,'gy'=4] {'gy'}, use_global_device_ids=true, to_apply=%region_69.0 | all-reduce | flops 6 | bytes 48 | tf_op jit(solution)/shard_map/psum | solution.py:17
  313.7 12.4 %all-reduce.5 = (f32[]{:T(128)}, f32[5]{0:T(128)S(1)}) all-reduce(f32[]{:T(128)} %get-tuple-element.169, f32[5]{0:T(128)S(1)} %get-tuple-element.170), channel_id=1, replica_groups=mesh['gx'=8,'gy'=4] {'gx'}, use_global_device_ids=true, to_apply=%region_70.0 | all-reduce | flops 6 | bytes 48 | tf_op jit(solution)/shard_map/psum | solution.py:17
  328.7 3.2 subtract_divide_fusion.13
  333.1 3.2 subtract_divide_fusion.4
  338.3 3.0 collective-permute-start.21
  352.0 4.5 collective-permute-start.23
  371.1 11.3 %all-reduce.14 = (f32[]{:T(128)}, f32[6]{0:T(128)S(1)}) all-reduce(f32[]{:T(128)S(6)} %add.739, f32[6]{0:T(128)S(1)} %stack.217), channel_id=1, replica_groups=mesh['gx'=8,'gy'=4] {'gy'}, use_global_device_ids=true, to_apply=%region_89.0 | all-reduce | flops 7 | bytes 56 | tf_op jit(solution)/shard_map/psum | solution.py:17
  382.4 12.6 %all-reduce.4 = (f32[]{:T(128)}, f32[6]{0:T(128)S(1)}) all-reduce(f32[]{:T(128)} %get-tuple-element.167, f32[6]{0:T(128)S(1)} %get-tuple-element.168), channel_id=1, replica_groups=mesh['gx'=8,'gy'=4] {'gx'}, use_global_device_ids=true, to_apply=%region_90.0 | all-reduce | flops 7 | bytes 56 | tf_op jit(solution)/shard_map/psum | solution.py:17
  397.6 3.7 subtract_divide_fusion.12
  403.2 3.8 subtract_divide_fusion.3
  411.7 3.0 collective-permute-start.25
  427.0 4.5 collective-permute-start.27
  448.3 11.3 %all-reduce.13 = (f32[]{:T(128)}, f32[7]{0:T(128)S(1)}) all-reduce(f32[]{:T(128)S(6)} %add.754, f32[7]{0:T(128)S(1)} %stack.225), channel_id=1, replica_groups=mesh['gx'=8,'gy'=4] {'gy'}, use_global_device_ids=true, to_apply=%region_111.0 | all-reduce | flops 8 | bytes 64 | tf_op jit(solution)/shard_map/psum | solution.py:17
  459.6 12.4 %all-reduce.3 = (f32[]{:T(128)}, f32[7]{0:T(128)S(1)}) all-reduce(f32[]{:T(128)} %get-tuple-element.165, f32[7]{0:T(128)S(1)} %get-tuple-element.166), channel_id=1, replica_groups=mesh['gx'=8,'gy'=4] {'gx'}, use_global_device_ids=true, to_apply=%region_112.0 | all-reduce | flops 8 | bytes 64 | tf_op jit(solution)/shard_map/psum | solution.py:17
  474.7 4.4 subtract_divide_fusion.11
  481.1 4.5 subtract_divide_fusion.2
  490.7 2.1 copy.529
  494.1 3.6 collective-permute-start.29
  497.7 2.1 pad_maximum_fusion.15
  511.6 4.5 collective-permute-start.31
  524.0 2.6 multiply_reduce_fusion.22
  538.0 11.2 %all-reduce.12 = (f32[]{:T(128)}, f32[8]{0:T(128)S(1)}) all-reduce(f32[]{:T(128)S(6)} %add.770, f32[8]{0:T(128)S(1)} %stack.234), channel_id=1, replica_groups=mesh['gx'=8,'gy'=4] {'gy'}, use_global_device_ids=true, to_apply=%region_135.0 | all-reduce | flops 9 | bytes 72 | tf_op jit(solution)/shard_map/psum | solution.py:17
  549.2 12.4 %all-reduce.2 = (f32[]{:T(128)}, f32[8]{0:T(128)S(1)}) all-reduce(f32[]{:T(128)} %get-tuple-element.163, f32[8]{0:T(128)S(1)} %get-tuple-element.164), channel_id=1, replica_groups=mesh['gx'=8,'gy'=4] {'gx'}, use_global_device_ids=true, to_apply=%region_136.0 | all-reduce | flops 9 | bytes 72 | tf_op jit(solution)/shard_map/psum | solution.py:17
  564.4 5.0 subtract_divide_fusion.10
  572.0 5.1 subtract_divide_fusion.1
  584.6 2.1 copy.530
  588.0 3.6 collective-permute-start.33
  591.6 2.1 pad_maximum_fusion.17
  599.9 1.9 concatenate.447
  604.9 4.8 collective-permute-start.35
  618.2 2.1 multiply_reduce_fusion.12
  632.9 11.1 %all-reduce.11 = (f32[]{:T(128)}, f32[9]{0:T(128)S(1)}) all-reduce(f32[]{:T(128)S(6)} %add.787, f32[9]{0:T(128)S(1)} %stack.244), channel_id=1, replica_groups=mesh['gx'=8,'gy'=4] {'gy'}, use_global_device_ids=true, to_apply=%region_161.0 | all-reduce | flops 10 | bytes 80 | tf_op jit(solution)/shard_map/psum | solution.py:17
  644.0 12.4 %all-reduce.1 = (f32[]{:T(128)}, f32[9]{0:T(128)S(1)}) all-reduce(f32[]{:T(128)} %get-tuple-element.161, f32[9]{0:T(128)S(1)} %get-tuple-element.162), channel_id=1, replica_groups=mesh['gx'=8,'gy'=4] {'gx'}, use_global_device_ids=true, to_apply=%region_162.0 | all-reduce | flops 10 | bytes 80 | tf_op jit(solution)/shard_map/psum | solution.py:17
  659.0 5.7 subtract_divide_fusion.9
  667.3 6.6 subtract_divide_fusion
  683.1 2.1 copy.531
  686.5 3.6 collective-permute-start.37
  690.1 2.0 pad_maximum_fusion.19
  704.9 4.5 collective-permute-start.39
  715.0 2.0 mul.2912
  718.7 2.1 multiply_reduce_fusion
  734.5 11.2 %all-reduce.10 = (f32[10]{0:T(128)S(1)}, f32[]{:T(128)}) all-reduce(f32[10]{0:T(128)S(1)} %stack.255, f32[]{:T(128)S(6)} %add.805), channel_id=1, replica_groups=mesh['gx'=8,'gy'=4] {'gy'}, use_global_device_ids=true, to_apply=%region_185.0 | all-reduce | flops 11 | bytes 88 | tf_op jit(solution)/shard_map/psum | solution.py:17
  745.7 12.4 %all-reduce = (f32[10]{0:T(128)S(1)}, f32[]{:T(128)}) all-reduce(f32[10]{0:T(128)S(1)} %get-tuple-element.159, f32[]{:T(128)} %get-tuple-element.160), channel_id=1, replica_groups=mesh['gx'=8,'gy'=4] {'gx'}, use_global_device_ids=true, to_apply=%region_186.0 | all-reduce | flops 11 | bytes 88 | tf_op jit(solution)/shard_map/psum | solution.py:17
  (502 shorter events, 171.3 us)
Async XLA Ops:
  0.6 4.4 copy-start.43
  2.0 50.2 %copy-start = (f32[2,16,2048]{2,1,0:T(8,128)S(1)}, f32[2,16,2048]{2,1,0:T(8,128)}, u32[]{:S(2)}) copy-start(f32[2,16,2048]{2,1,0:T(8,128)} %param.5) | copy-start | bytes 786436
  47.9 8.4 %collective-permute-start = (f32[1,16,33]{1,0,2:T(1,128)S(1)}, f32[1,16,33]{1,0,2:T(1,128)S(1)}, u32[]{:S(2)}, u32[]{:S(2)}) collective-permute-start(f32[1,16,33]{1,0,2:T(1,128)S(1)} %get-tuple-element.352), channel_id=1, source_target_pairs={{4,0},{8,4},{12,8},{16,12},{20,16},{24,20},{28,24},{5,1},{9,5},{13... | collective-permute-start | bytes 6344 | tf_op jit(solution)/shard_map/ppermute | solution.py:31
  49.2 7.1 collective-permute-start.1
  56.4 6.2 collective-permute-start.2
  57.7 6.5 collective-permute-start.3
  99.4 7.8 collective-permute-start.4
  100.7 6.5 collective-permute-start.5
  107.3 6.8 collective-permute-start.6
  108.6 6.9 collective-permute-start.7
  152.2 8.4 %collective-permute-start.8 = (f32[1,16,33]{1,0,2:T(1,128)S(1)}, f32[1,16,33]{1,0,2:T(1,128)S(1)}, u32[]{:S(2)}, u32[]{:S(2)}) collective-permute-start(f32[1,16,33]{1,0,2:T(1,128)S(1)} %get-tuple-element.338), channel_id=1, source_target_pairs={{4,0},{8,4},{12,8},{16,12},{20,16},{24,20},{28,24},{5,1},{9,5},{13... | collective-permute-start | bytes 6344 | tf_op jit(solution)/shard_map/ppermute | solution.py:31
  153.5 7.1 collective-permute-start.9
  160.7 6.8 collective-permute-start.10
  162.0 6.9 collective-permute-start.11
  209.7 9.5 %collective-permute-start.12 = (f32[1,16,33]{1,0,2:T(1,128)S(1)}, f32[1,16,33]{1,0,2:T(1,128)S(1)}, u32[]{:S(2)}, u32[]{:S(2)}) collective-permute-start(f32[1,16,33]{1,0,2:T(1,128)S(1)} %get-tuple-element.331), channel_id=1, source_target_pairs={{4,0},{8,4},{12,8},{16,12},{20,16},{24,20},{28,24},{5,1},{9,5},{13... | collective-permute-start | bytes 6344 | tf_op jit(solution)/shard_map/ppermute | solution.py:31
  211.0 8.2 %collective-permute-start.13 = (f32[1,16,33]{1,0,2:T(1,128)S(1)}, f32[1,16,33]{1,0,2:T(1,128)S(1)}, u32[]{:S(2)}, u32[]{:S(2)}) collective-permute-start(f32[1,16,33]{1,0,2:T(1,128)S(1)} %get-tuple-element.330), channel_id=1, source_target_pairs={{0,4},{4,8},{8,12},{12,16},{16,20},{20,24},{24,28},{1,5},{5,9},{9,... | collective-permute-start | bytes 6344 | tf_op jit(solution)/shard_map/ppermute | solution.py:29
  219.4 6.8 collective-permute-start.14
  220.7 6.9 collective-permute-start.15
  225.6 2.3 copy-start.42
  271.3 11.7 %collective-permute-start.16 = (f32[1,16,33]{1,0,2:T(1,128)}, f32[1,16,33]{1,0,2:T(1,128)S(1)}, u32[]{:S(2)}, u32[]{:S(2)}) collective-permute-start(f32[1,16,33]{1,0,2:T(1,128)} %get-tuple-element.324), channel_id=1, source_target_pairs={{4,0},{8,4},{12,8},{16,12},{20,16},{24,20},{28,24},{5,1},{9,5},{13... | collective-permute-start | bytes 6344 | tf_op jit(solution)/shard_map/ppermute | solution.py:31
  272.6 10.4 %collective-permute-start.17 = (f32[1,16,33]{1,0,2:T(1,128)}, f32[1,16,33]{1,0,2:T(1,128)S(1)}, u32[]{:S(2)}, u32[]{:S(2)}) collective-permute-start(f32[1,16,33]{1,0,2:T(1,128)} %get-tuple-element.323), channel_id=1, source_target_pairs={{0,4},{4,8},{8,12},{12,16},{16,20},{20,24},{24,28},{1,5},{5,9},{9,... | collective-permute-start | bytes 6344 | tf_op jit(solution)/shard_map/ppermute | solution.py:29
  283.2 6.8 collective-permute-start.18
  284.5 6.9 collective-permute-start.19
  289.4 2.3 copy-start.41
  337.0 13.5 %collective-permute-start.20 = (f32[1,16,33]{1,0,2:T(1,128)S(1)}, f32[1,16,33]{1,0,2:T(1,128)S(1)}, u32[]{:S(2)}, u32[]{:S(2)}) collective-permute-start(f32[1,16,33]{1,0,2:T(1,128)S(1)} %get-tuple-element.317), channel_id=1, source_target_pairs={{4,0},{8,4},{12,8},{16,12},{20,16},{24,20},{28,24},{5,1},{9,5},{13... | collective-permute-start | bytes 6344 | tf_op jit(solution)/shard_map/ppermute | solution.py:31
  338.3 12.2 %collective-permute-start.21 = (f32[1,16,33]{1,0,2:T(1,128)S(1)}, f32[1,16,33]{1,0,2:T(1,128)S(1)}, u32[]{:S(2)}, u32[]{:S(2)}) collective-permute-start(f32[1,16,33]{1,0,2:T(1,128)S(1)} %get-tuple-element.316), channel_id=1, source_target_pairs={{0,4},{4,8},{8,12},{12,16},{16,20},{20,24},{24,28},{1,5},{5,9},{9,... | collective-permute-start | bytes 6344 | tf_op jit(solution)/shard_map/ppermute | solution.py:29
  343.6 6.7 copy-start.9
  350.7 6.8 collective-permute-start.22
  352.0 6.9 collective-permute-start.23
  356.9 2.3 copy-start.30
  356.9 2.3 copy-start.39
  356.9 2.3 copy-start.40
  410.4 15.2 %collective-permute-start.24 = (f32[1,16,33]{1,0,2:T(1,128)}, f32[1,16,33]{1,0,2:T(1,128)S(1)}, u32[]{:S(2)}, u32[]{:S(2)}) collective-permute-start(f32[1,16,33]{1,0,2:T(1,128)} %get-tuple-element.309), channel_id=1, source_target_pairs={{4,0},{8,4},{12,8},{16,12},{20,16},{24,20},{28,24},{5,1},{9,5},{13... | collective-permute-start | bytes 6344 | tf_op jit(solution)/shard_map/ppermute | solution.py:31
  411.7 13.9 %collective-permute-start.25 = (f32[1,16,33]{1,0,2:T(1,128)}, f32[1,16,33]{1,0,2:T(1,128)S(1)}, u32[]{:S(2)}, u32[]{:S(2)}) collective-permute-start(f32[1,16,33]{1,0,2:T(1,128)} %get-tuple-element.308), channel_id=1, source_target_pairs={{0,4},{4,8},{8,12},{12,16},{16,20},{20,24},{24,28},{1,5},{5,9},{9,... | collective-permute-start | bytes 6344 | tf_op jit(solution)/shard_map/ppermute | solution.py:29
  425.7 6.8 collective-permute-start.26
  427.0 6.9 collective-permute-start.27
  431.9 2.3 copy-start.29
  432.0 2.3 copy-start.37
  432.0 2.4 copy-start.38
  474.7 6.4 copy-start.23
  488.1 9.5 %copy-start.3 = (f32[2,16,32,1]{3,2,1,0:T(8,128)S(1)}, f32[2,16,32,1]{3,2,1,0:T(8,128)}, u32[]{:S(2)}) copy-start(f32[2,16,32,1]{3,2,1,0:T(8,128)} %get-tuple-element.217) | copy-start | bytes 12292
  492.8 16.6 %collective-permute-start.28 = (f32[1,16,33]{1,0,2:T(1,128)}, f32[1,16,33]{1,0,2:T(1,128)S(1)}, u32[]{:S(2)}, u32[]{:S(2)}) collective-permute-start(f32[1,16,33]{1,0,2:T(1,128)} %get-tuple-element.300), channel_id=1, source_target_pairs={{4,0},{8,4},{12,8},{16,12},{20,16},{24,20},{28,24},{5,1},{9,5},{13... | collective-permute-start | bytes 6344 | tf_op jit(solution)/shard_map/ppermute | solution.py:31
  494.1 15.3 %collective-permute-start.29 = (f32[1,16,33]{1,0,2:T(1,128)}, f32[1,16,33]{1,0,2:T(1,128)}, u32[]{:S(2)}, u32[]{:S(2)}) collective-permute-start(f32[1,16,33]{1,0,2:T(1,128)} %get-tuple-element.299), channel_id=1, source_target_pairs={{0,4},{4,8},{8,12},{12,16},{16,20},{20,24},{24,28},{1,5},{5,9},{9,... | collective-permute-start | bytes 6344 | tf_op jit(solution)/shard_map/ppermute | solution.py:29
  497.7 2.1 copy-start.12
  497.7 2.1 copy-start.13
  500.8 7.6 copy-start.8
  510.3 7.0 collective-permute-start.30
  511.6 6.5 collective-permute-start.31
  564.3 7.6 copy-start.19
  579.6 12.0 %copy-start.2 = (f32[2,16,32,1]{3,2,1,0:T(8,128)S(1)}, f32[2,16,32,1]{3,2,1,0:T(8,128)}, u32[]{:S(2)}) copy-start(f32[2,16,32,1]{3,2,1,0:T(8,128)} %get-tuple-element.213) | copy-start | bytes 12292
  586.7 16.0 %collective-permute-start.32 = (f32[1,16,33]{1,0,2:T(1,128)}, f32[1,16,33]{1,0,2:T(1,128)}, u32[]{:S(2)}, u32[]{:S(2)}) collective-permute-start(f32[1,16,33]{1,0,2:T(1,128)} %get-tuple-element.290), channel_id=1, source_target_pairs={{4,0},{8,4},{12,8},{16,12},{20,16},{24,20},{28,24},{5,1},{9,5},{13... | collective-permute-start | bytes 6344 | tf_op jit(solution)/shard_map/ppermute | solution.py:31
  588.0 14.7 %collective-permute-start.33 = (f32[1,16,33]{1,0,2:T(1,128)}, f32[1,16,33]{1,0,2:T(1,128)}, u32[]{:S(2)}, u32[]{:S(2)}) collective-permute-start(f32[1,16,33]{1,0,2:T(1,128)} %get-tuple-element.289), channel_id=1, source_target_pairs={{0,4},{4,8},{8,12},{12,16},{16,20},{20,24},{24,28},{1,5},{5,9},{9,... | collective-permute-start | bytes 6344 | tf_op jit(solution)/shard_map/ppermute | solution.py:29
  591.6 2.1 copy-start.10
  591.6 2.1 copy-start.11
  594.8 7.0 copy-start.7
  603.6 7.9 %collective-permute-start.34 = (f32[4,1,33]{1,0,2:T(4,128)S(1)}, f32[4,1,33]{1,0,2:T(4,128)S(1)}, u32[]{:S(2)}, u32[]{:S(2)}) collective-permute-start(f32[4,1,33]{1,0,2:T(4,128)S(1)} %get-tuple-element.250), channel_id=1, source_target_pairs={{1,0},{2,1},{3,2},{5,4},{6,5},{7,6},{9,8},{10,9},{11,10},{13,12},{... | collective-permute-start | bytes 1592 | tf_op jit(solution)/shard_map/ppermute | solution.py:31
  604.9 6.6 collective-permute-start.35
  632.9 26.1 %copy-start.24 = (f32[2,16,32]{1,0,2:T(2,128)S(1)}, f32[2,16,32]{1,0,2:T(2,128)}, u32[]{:S(2)}) copy-start(f32[2,16,32]{1,0,2:T(2,128)} %get-tuple-element.181) | copy-start | bytes 12292
  677.4 12.7 %copy-start.1 = (f32[2,16,32,1]{3,2,1,0:T(8,128)S(1)}, f32[2,16,32,1]{3,2,1,0:T(8,128)}, u32[]{:S(2)}) copy-start(f32[2,16,32,1]{3,2,1,0:T(8,128)} %get-tuple-element.209) | copy-start | bytes 12292
  685.2 17.0 %collective-permute-start.36 = (f32[1,16,33]{1,0,2:T(1,128)}, f32[1,16,33]{1,0,2:T(1,128)}, u32[]{:S(2)}, u32[]{:S(2)}) collective-permute-start(f32[1,16,33]{1,0,2:T(1,128)} %get-tuple-element.279), channel_id=1, source_target_pairs={{4,0},{8,4},{12,8},{16,12},{20,16},{24,20},{28,24},{5,1},{9,5},{13... | collective-permute-start | bytes 6344 | tf_op jit(solution)/shard_map/ppermute | solution.py:31
  686.5 15.7 %collective-permute-start.37 = (f32[1,16,33]{1,0,2:T(1,128)}, f32[1,16,33]{1,0,2:T(1,128)}, u32[]{:S(2)}, u32[]{:S(2)}) collective-permute-start(f32[1,16,33]{1,0,2:T(1,128)} %get-tuple-element.278), channel_id=1, source_target_pairs={{0,4},{4,8},{8,12},{12,16},{16,20},{20,24},{24,28},{1,5},{5,9},{9,... | collective-permute-start | bytes 6344 | tf_op jit(solution)/shard_map/ppermute | solution.py:29
  703.6 7.7 collective-permute-start.38
  704.9 6.5 collective-permute-start.39
  715.0 3.7 copy-start.20
  (39 other events, 42.8 us)
